TPU v7x, 32 devices: a whole 2x2x4 slice. The times are simulated.
32 devices in a mesh: root: 4 (over z), virt: 4 (over y, x), occ: 2 (over core).
Axes of the slice: x: 2, y: 2, z: 4, core: 2. Of those that a mesh axis runs over, the one named last changes fastest.
Arguments:
- trial_singles: bfloat16 [8, 96], P('root'), may hold values from -6 to 6
- trial_doubles: bfloat16 [8, 480, 9216], P('root', 'virt', 'occ'), may hold values from -6 to 6
- occ_fock: bfloat16 [96, 96], replicated, may hold values from -0.625 to 0.625
- virt_fock: bfloat16 [480, 480], replicated, may hold values from -0.25 to 0.25
- w_ovoo: bfloat16 [96, 480, 9216], P('occ', 'virt', 'root'), may hold values from -0.625 to 0.625
- w_ooov: bfloat16 [96, 480, 9216], P('occ', 'virt', 'root'), may hold values from -0.0029296875 to 0.0029296875
- converged: int32 [8], replicated, may hold values from 0 to 1, as said below
Outputs:
- sigma_doubles: bfloat16 [8, 480, 9216], P('root', 'virt', 'occ')
- sigma_singles: float32 [8, 96], P('root')
- subspace: float32 [8, 8], P('root')
Inputs may be any that keep to these rules, and one draw needn't show every extreme that they name: `converged`: exactly 4 roots are active (0). In every draw at least one aligned block of 2 roots has all its roots active; other blocks may have none.
All inputs are finite; a program needn't handle non-finite values.
Results may differ from a plain program's by a relative error of at most 0.0044.
Values may be sent and summed in bfloat16 or wider, within the bound.
A program may use at most 256 MiB of HBM per device.

v0:
```python
import math
import jax
import jax.numpy as jnp
from jax import lax
from jax.sharding import PartitionSpec as P


def flat_pairs(left, right):
    return lax.dot_general(
        left.reshape(left.shape[0], -1),
        right.reshape(right.shape[0], -1),
        (((1,), (1,)), ((), ())),
        preferred_element_type=jnp.float32,
    )


def local(trial_singles, trial_doubles, occ_fock, virt_fock, w_ovoo, w_ooov, converged):
    local_roots, virt_local, pair_local = trial_doubles.shape
    occ_count = occ_fock.shape[0]
    virt_count = virt_fock.shape[0]
    root_count = converged.shape[0]
    root_groups = lax.axis_size("root")
    occ_groups = lax.axis_size("occ")
    root_index = lax.axis_index("root")
    occ_index = lax.axis_index("occ")
    occ_half = occ_count // occ_groups
    block_pairs = occ_count * occ_count // root_groups
    own_start = occ_index * occ_half
    active = (1 - converged).astype(jnp.float32)
    own_active = lax.dynamic_slice_in_dim(active, root_index * local_roots, local_roots)
    singles_all = lax.all_gather(trial_singles, "root", axis=0, tiled=True)
    gathered = lax.all_gather(trial_doubles, "occ", axis=2, tiled=True)
    fock_cols = lax.dynamic_slice_in_dim(occ_fock, own_start, occ_half, 1)
    batch_rows = local_roots * virt_local
    stacked = gathered.reshape(batch_rows, occ_count, occ_count)
    first_term = jnp.einsum(
        "ki,bkj->bij", fock_cols, stacked, preferred_element_type=jnp.float32
    ).reshape(local_roots, virt_local, pair_local)
    own_rows = trial_doubles.reshape(batch_rows, occ_half, occ_count)
    second_term = jnp.einsum(
        "bik,kj->bij", own_rows, occ_fock, preferred_element_type=jnp.float32
    ).reshape(local_roots, virt_local, pair_local)
    doubles_block = lax.all_to_all(gathered, "root", split_axis=2, concat_axis=0, tiled=True)
    partial_coupling = flat_pairs(doubles_block, w_ooov)
    coupling_part = lax.dynamic_update_slice(
        jnp.zeros((root_count, occ_count), jnp.float32), partial_coupling, (jnp.int32(0), own_start)
    )
    coupling = lax.psum(coupling_part, ("root", "virt", "occ"))
    singles_fock = jnp.dot(singles_all, occ_fock, preferred_element_type=jnp.float32)
    singles_every = active[:, None] * (-singles_fock - 0.5 * coupling)
    sigma_singles = lax.dynamic_slice_in_dim(singles_every, root_index * local_roots, local_roots)
    singles_cols = lax.dynamic_slice_in_dim(singles_all, own_start, occ_half, 1)
    outer_part = (
        -jnp.dot(singles_cols, w_ovoo.reshape(occ_half, -1), preferred_element_type=jnp.float32)
    ).reshape(root_count, virt_local, block_pairs)
    product = jnp.einsum(
        "ac,ncp->nap",
        virt_fock,
        lax.all_to_all(trial_doubles, "virt", split_axis=2, concat_axis=1, tiled=True),
        preferred_element_type=jnp.float32,
    ).astype(jnp.bfloat16)
    vv_term = lax.all_to_all(product, "virt", split_axis=1, concat_axis=2, tiled=True)
    vv_value = vv_term.astype(jnp.float32)
    outer_own = lax.all_to_all(outer_part, "root", split_axis=0, concat_axis=2, tiled=True)
    outer_half = lax.psum_scatter(outer_own, "occ", scatter_dimension=2, tiled=True)
    summed = vv_value + outer_half - first_term - second_term
    sigma_doubles = (own_active[:, None, None] * summed).astype(jnp.bfloat16)
    trial_piece, sigma_piece = (
        lax.all_to_all(trial_doubles, "root", split_axis=2, concat_axis=0, tiled=True),
        lax.all_to_all(sigma_doubles, "root", split_axis=2, concat_axis=0, tiled=True),
    )
    doubles_part = lax.psum(flat_pairs(trial_piece, sigma_piece), ("root", "virt", "occ"))
    singles_part = jnp.dot(
        singles_all.astype(jnp.float32), singles_every.T, precision=lax.Precision.HIGHEST
    )
    whole_matrix = doubles_part / math.sqrt(
        occ_count * occ_count * virt_count
    ) + singles_part / math.sqrt(occ_count)
    subspace = lax.dynamic_slice_in_dim(whole_matrix, root_index * local_roots, local_roots, 0)
    return (sigma_doubles, sigma_singles, subspace)


def solution(mesh):
    placed = (
        P("root", None),
        P("root", "virt", "occ"),
        P(),
        P(),
        P("occ", "virt", "root"),
        P("occ", "virt", "root"),
        P(),
    )
    return jax.shard_map(
        local,
        mesh=mesh,
        in_specs=placed,
        out_specs=(P("root", "virt", "occ"), P("root", None), P("root", None)),
        check_vma=False,
    )
```

profile of v0, /device:TPU:0, one launch (start us, length us, event | category | flops | bytes accessed | tf_op | source)
XLA Modules:
  0.0 595.7 jit_solution(10986336026013833331)
XLA Ops:
  7.2 6.9 %copy.53 = bf16[2,120,4608]{1,0,2:T(2,128)(2,1)} copy(bf16[2,120,4608]{2,1,0:T(8,128)(2,1)} %param.8) | data formatting | bytes 4423680 | tf_op args[1]
  14.1 5.2 all-to-all-start
  19.3 24.4 %copy.79 = bf16[6,8,120,2304]{3,1,2,0:T(8,128)(2,1)} copy(bf16[6,8,120,2304]{3,2,1,0:T(8,128)(2,1)} %bitcast.88) | data formatting | bytes 53084160
  43.7 11.1 %all-gather = bf16[4,2,96]{2,1,0:T(2,128)(2,1)S(1)} all-gather(bf16[1,2,96]{2,1,0:T(2,128)(2,1)S(1)} %bitcast.102), channel_id=1, replica_groups=mesh['root'=4,'virt'=4,'occ'=2] {'root'}, dimensions={0}, use_global_device_ids=true | all-gather | bytes 1920 | tf_op jit(solution)/shard_map/all_gather | solution.py:31
  54.8 10.4 %convolution_negate_fusion = f32[8,276480]{1,0:T(8,128)S(1)} fusion(bf16[48,276480]{1,0:T(8,128)(2,1)} %bitcast.84, bf16[8,96]{1,0:T(8,128)(2,1)S(1)} %bitcast.99, s32[]{:T(128)S(6)} %select_n.5), kind=kOutput, calls=%fused_computation | convolution fusion | flops 214548480 | bytes 35390980 | tf_op jit(solution)/shard_map/dot_general | solution.py:54
  65.3 6.1 %copy.57 = f32[8,120,2304]{2,1,0:T(8,128)} copy(f32[8,120,2304]{2,0,1:T(8,128)S(1)} %bitcast.85) | data formatting | bytes 17694720 | tf_op jit(solution)/shard_map/reshape | solution.py:55
  71.4 5.7 all-to-all-start.2
  77.2 0.7 all-gather.3.cloned.1.call-update
  77.8 4.4 copy.54
  82.2 2.9 fusion.4
  85.2 3.1 copy.55
  88.3 180.0 %all-to-all-done.2 = f32[8,120,2304]{2,1,0:T(8,128)} async-done(((f32[8,120,2304]{2,1,0:T(8,128)}), f32[8,120,2304]{2,1,0:T(8,128)}, u32[]{:S(2)}, u32[]{:S(2)}) %all-to-all-start.2) | async-done | bytes 8847392 | tf_op jit(solution)/shard_map/all_to_all | solution.py:64
  268.2 3.9 all-to-all-start.1
  272.1 14.5 %copy.58 = f32[2,120,4,2304]{1,0,3,2:T(2,128)} copy(f32[2,120,4,2304]{3,1,0,2:T(8,128)} %bitcast.12) | data formatting | bytes 17694720 | tf_op jit(solution)/shard_map/all_to_all | solution.py:64
  286.6 10.8 %all-to-all-done.1 = bf16[2,480,1152]{2,0,1:T(2,128)(2,1)S(1)} async-done(((bf16[2,480,1152]{2,0,1:T(2,128)(2,1)}), bf16[2,480,1152]{2,0,1:T(2,128)(2,1)S(1)}, u32[]{:S(2)}, u32[]{:S(2)}) %all-to-all-start.1) | async-done | bytes 2211872 | tf_op jit(solution)/shard_map/all_to_all | solution.py:62
  297.5 1.4 copy-done.2
  298.8 3.7 all-to-all-start.5
  302.6 12.7 %copy.65 = bf16[2,120,9216]{1,0,2:T(2,128)(2,1)} copy(bf16[2,120,9216]{2,1,0:T(8,128)(2,1)} %all-gather.3.cloned.1.call-done) | data formatting | bytes 8847360 | tf_op jit(solution)/shard_map/all_gather | solution.py:32
  315.3 40.6 %all-to-all-done.5 = bf16[2,120,4608]{1,0,2:T(2,128)(2,1)S(1)} async-done(((bf16[2,120,4608]{1,0,2:T(2,128)(2,1)}), bf16[2,120,4608]{1,0,2:T(2,128)(2,1)S(1)}, u32[]{:S(2)}, u32[]{:S(2)}) %all-to-all-start.5) | async-done | bytes 2211872 | tf_op jit(solution)/shard_map/all_to_all | solution.py:69
  356.0 5.1 all-to-all-start.3
  361.1 5.9 reshape.49
  367.0 4.7 fusion.11
  371.6 7.1 %reshape.50 = f32[2,120,4608]{1,0,2:T(2,128)} reshape(f32[240,48,96]{0,2,1:T(8,128)} %fusion.11) | data formatting | bytes 8847360 | tf_op jit(solution)/shard_map/reshape | solution.py:42
  378.9 0.6 dynamic-slice
  380.1 8.9 %copy.56 = f32[2,4,120,1152]{2,0,3,1:T(2,128)} copy(bf16[2,4,120,1152]{3,0,2,1:T(2,128)(2,1)} %bitcast.95) | data formatting | bytes 6635520 | tf_op jit(solution)/shard_map/convert_element_type | solution.py:63
  389.0 9.5 %reshape.62 = bf16[240,96,96]{2,1,0:T(8,128)(2,1)} reshape(bf16[2,120,9216]{2,1,0:T(8,128)(2,1)} %all-gather.3.cloned.1.call-done) | data formatting | bytes 8847360 | tf_op jit(solution)/shard_map/reshape | solution.py:35
  398.6 9.2 %copy.61 = bf16[240,96,96]{0,1,2:T(8,128)(2,1)} copy(bf16[240,96,96]{2,1,0:T(8,128)(2,1)} %reshape.62) | data formatting | bytes 8847360 | tf_op jit(solution)/shard_map/reshape | solution.py:35
  407.8 3.2 convolution_bitcast_fusion
  411.0 4.8 copy.62
  415.9 7.1 %reshape.48 = f32[2,120,4608]{1,0,2:T(2,128)} reshape(f32[240,48,96]{0,2,1:T(8,128)} %copy.62) | data formatting | bytes 8847360 | tf_op jit(solution)/shard_map/reshape | solution.py:38
  423.0 10.2 %fusion.3 = bf16[2,120,4608]{1,0,2:T(2,128)(2,1)} fusion(f32[2,120,4608]{1,0,2:T(2,128)} %reshape.50, f32[2,120,4608]{1,0,2:T(2,128)} %reshape.48, f32[2,120,9216]{1,0,2:T(2,128)} %all-reduce.4.cloned.1.call-done, u32[]{:T(128)S(6)} %multiply.4, f32[2,4,120,1152]{2,0,3,1:T(2,128)} %copy.56, f32[2]{0:T(128)S(1)} %dynamic_slice.15), kind=kLoop, calls=%fused_computation.5 | loop fusion | flops 5529600 | bytes 19906572 | tf_op jit(solution)/shard_map/convert_element_type | solution.py:67
  433.2 31.7 %all-to-all-done.3 = bf16[2,120,9216]{1,0,2:T(2,128)(2,1)} async-done(((bf16[2,120,9216]{1,0,2:T(2,128)(2,1)}), bf16[2,120,9216]{1,0,2:T(2,128)(2,1)}, u32[]{:S(2)}, u32[]{:S(2)}) %all-to-all-start.3) | async-done | bytes 4423712 | tf_op jit(solution)/shard_map/all_to_all | solution.py:43
  464.9 4.7 all-to-all-start.4
  469.6 24.4 %copy.81 = bf16[6,8,120,2304]{3,1,2,0:T(8,128)(2,1)} copy(bf16[6,8,120,2304]{3,2,1,0:T(8,128)(2,1)} %bitcast.89) | data formatting | bytes 53084160
  494.0 4.3 copy.69
  498.3 1.9 copy.83
  500.2 12.3 %copy.66 = bf16[2,120,4,2304]{3,1,0,2:T(8,128)(2,1)} copy(bf16[2,120,4,2304]{1,0,3,2:T(2,128)(2,1)} %bitcast.17) | data formatting | bytes 8847360 | tf_op jit(solution)/shard_map/all_to_all | solution.py:43
  512.5 5.2 copy.80
  517.7 13.4 %fusion.17 = f32[8,48]{1,0:T(8,128)S(1)} fusion(bf16[8,276480]{1,0:T(8,128)(2,1)} %bitcast.87, bf16[48,276480]{1,0:T(8,128)(2,1)} %bitcast.83), kind=kOutput, calls=%fused_computation.27 | convolution fusion | flops 212336640 | bytes 30967296 | tf_op jit(solution)/shard_map/dot_general | solution.py:9
  531.0 0.2 dynamic_update_slice.3
  531.2 6.7 %copy.71 = bf16[2,120,4608]{2,1,0:T(8,128)(2,1)} copy(bf16[2,120,4608]{1,0,2:T(2,128)(2,1)} %fusion.3) | data formatting | bytes 4423680
  537.9 6.8 %copy.67 = bf16[2,120,4,1152]{3,1,0,2:T(8,128)(2,1)} copy(bf16[2,120,4,1152]{1,0,3,2:T(2,128)(2,1)} %bitcast.19) | data formatting | bytes 4423680 | tf_op jit(solution)/shard_map/all_to_all | solution.py:70
  544.7 1.9 copy.82
  546.6 1.2 convolution_bitcast_fusion.1
  547.8 39.5 %all-reduce.1 = (f32[8,96]{1,0:T(8,128)S(1)}, f32[8,8]{0,1:T(8,128)S(1)}) all-reduce(f32[8,96]{1,0:T(8,128)S(1)} %dynamic_update_slice.3, f32[8,8]{0,1:T(8,128)S(1)} %convolution_bitcast_fusion.1), channel_id=1, replica_groups=mesh['root'=4,'virt'=4,'occ'=2] {'root','virt','occ'}, use_global_device_ids=true, to_apply=%region_1.0 | all-reduce | flops 832 | bytes 6656 | tf_op jit(solution)/shard_map/psum | solution.py:48
  587.4 0.6 constant_dynamic-slice_fusion.1
  588.0 0.1 fusion.6
  588.2 0.7 copy.72
  (25 shorter events, 0.3 us)
Async XLA Ops:
  7.2 75.1 %copy-start = (bf16[480,480]{1,0:T(8,128)(2,1)S(1)}, bf16[480,480]{1,0:T(8,128)(2,1)}, u32[]{:S(2)}) copy-start(bf16[480,480]{1,0:T(8,128)(2,1)} %param.10) | copy-start | bytes 1382404
  14.1 57.3 %all-to-all-start = ((bf16[2,120,4608]{1,0,2:T(2,128)(2,1)}), bf16[2,120,4608]{1,0,2:T(2,128)(2,1)S(1)}, u32[]{:S(2)}, u32[]{:S(2)}) async-start(bf16[2,120,4608]{1,0,2:T(2,128)(2,1)} %copy.53), calls=%async_computation | async-start | bytes 4718592 | tf_op jit(solution)/shard_map/all_to_all | solution.py:59
  19.3 24.4 %copy-start.4 = (bf16[2,96]{1,0:T(2,128)(2,1)S(1)}, bf16[2,96]{1,0:T(2,128)(2,1)}, u32[]{:S(2)}) copy-start(bf16[2,96]{1,0:T(2,128)(2,1)} %param.7) | copy-start | bytes 1156
  71.4 196.8 %all-to-all-start.2 = ((f32[8,120,2304]{2,1,0:T(8,128)}), f32[8,120,2304]{2,1,0:T(8,128)}, u32[]{:S(2)}, u32[]{:S(2)}) async-start(f32[8,120,2304]{2,1,0:T(8,128)} %copy.57), calls=%async_computation.2 | async-start | bytes 17694720 | tf_op jit(solution)/shard_map/all_to_all | solution.py:64
  77.1 225.4 %all-gather.3.cloned.1.call-start = ((), (), s32[]{:S(2)}) async-start(), calls=%async_computation.6 | async-start | bytes 6635520 | tf_op jit(solution)/shard_map/all_gather | solution.py:32
  268.2 29.2 %all-to-all-start.1 = ((bf16[2,480,1152]{2,0,1:T(2,128)(2,1)}), bf16[2,480,1152]{2,0,1:T(2,128)(2,1)S(1)}, u32[]{:S(2)}, u32[]{:S(2)}) async-start(bf16[2,480,1152]{2,0,1:T(2,128)(2,1)} %copy.55), calls=%async_computation.1 | async-start | bytes 4423680 | tf_op jit(solution)/shard_map/all_to_all | solution.py:62
  272.1 150.9 %all-reduce.4.cloned.1.call-start = ((), (), s32[]{:S(2)}) async-start(), calls=%async_computation.7 | async-start | bytes 18874368
  297.5 1.4 copy-start.2
  298.8 57.1 %all-to-all-start.5 = ((bf16[2,120,4608]{1,0,2:T(2,128)(2,1)}), bf16[2,120,4608]{1,0,2:T(2,128)(2,1)S(1)}, u32[]{:S(2)}, u32[]{:S(2)}) async-start(bf16[2,120,4608]{1,0,2:T(2,128)(2,1)} %copy.53), calls=%async_computation.5 | async-start | bytes 4718592 | tf_op jit(solution)/shard_map/all_to_all | solution.py:69
  356.0 108.9 %all-to-all-start.3 = ((bf16[2,120,9216]{1,0,2:T(2,128)(2,1)}), bf16[2,120,9216]{1,0,2:T(2,128)(2,1)}, u32[]{:S(2)}, u32[]{:S(2)}) async-start(bf16[2,120,9216]{1,0,2:T(2,128)(2,1)} %copy.65), calls=%async_computation.3 | async-start | bytes 9437184 | tf_op jit(solution)/shard_map/all_to_all | solution.py:43
  361.1 5.9 copy-start.3
  371.6 7.2 %copy-start.5 = (s32[8]{0:T(128)S(1)}, s32[8]{0:T(128)}, u32[]{:S(2)}) copy-start(s32[8]{0:T(128)} %param.13) | copy-start | bytes 100
  371.6 7.2 %copy-start.6 = (u32[32]{0:T(128)S(1)}, u32[32]{0:T(128)}, u32[]{:S(2)}) copy-start(u32[32]{0:T(128)} %constant.35) | copy-start | bytes 388
  464.9 73.0 %all-to-all-start.4 = ((bf16[2,120,4608]{1,0,2:T(2,128)(2,1)}), bf16[2,120,4608]{1,0,2:T(2,128)(2,1)}, u32[]{:S(2)}, u32[]{:S(2)}) async-start(bf16[2,120,4608]{1,0,2:T(2,128)(2,1)} %fusion.3), calls=%async_computation.4 | async-start | bytes 4718592 | tf_op jit(solution)/shard_map/all_to_all | solution.py:70
  537.9 51.0 %copy-start.1 = (bf16[480,480]{1,0:T(8,128)(2,1)S(1)}, bf16[480,480]{1,0:T(8,128)(2,1)}, u32[]{:S(2)}) copy-start(bf16[480,480]{1,0:T(8,128)(2,1)} %param.10) | copy-start | bytes 1382404
Sparse Core Ops, SparseCore 0:
  79.5 15.8 all-gather.2
  286.7 40.7 all-reduce.3
where the time goes:
time: 599 us; the launch traced here: 596 us
  waiting for transfers between devices  264 us (44%)
  local copies, waits for them, and re-layouts  192 us (32%)
  blocking collectives  50.7 us (8%)
  matrix products  36.1 us (6%)
  starting transfers between devices  28.3 us (5%)
  between operations  14.8 us (2%)
  other arithmetic  10.2 us (2%)
    all_to_all x1, waiting for transfers between devices, local(): lax.all_to_all(outer_part, 'root', split_axis=0, concat_axis=2, tiled=True)  180 us
    unnamed x23, local copies, waits for them, and re-layouts  74 us
    all_to_all x1, waiting for transfers between devices, local(): lax.all_to_all(trial_doubles, 'root', split_axis=2, concat_axis=0, tiled=...  40.6 us
    psum x1, blocking collectives, local(): coupling = lax.psum(coupling_part, ('root', 'virt', 'occ'))  39.5 us
    all_to_all x1, waiting for transfers between devices, local(): lax.all_to_all(gathered, 'root', split_axis=2, concat_axis=0, tiled=True)  31.7 us
    reshape x2, local copies, waits for them, and re-layouts, local(): stacked = gathered.reshape(batch_rows, occ_count, occ_count)  18.8 us
    dot_general x2, matrix products, flat_pairs(): lax.dot_general(left.reshape(left.shape[0], -1), right.reshape(right.shap...  14.6 us
    all_to_all x1, local copies, waits for them, and re-layouts, local(): lax.all_to_all(outer_part, 'root', split_axis=0, concat_axis=2, tiled=True)  14.5 us
  transfers between devices with their start and end apart: 8, of which 4 were waited for; matrix products, arithmetic and copies ran while one was open for 37% of the time, Pallas kernels for 0%

commit v1 on v0

--- a/solution.py
+++ b/solution.py
@@ -3,6 +3,11 @@
 import jax.numpy as jnp
 from jax import lax
 from jax.sharding import PartitionSpec as P
+
+
+def _manage_patches(mine_x, axis_key, axis_tag):
+    block_last = lax.psum(mine_x, axis_key)
+    return lax.psum(block_last, axis_tag)
 
 
 def flat_pairs(left, right):
@@ -45,7 +50,7 @@
     coupling_part = lax.dynamic_update_slice(
         jnp.zeros((root_count, occ_count), jnp.float32), partial_coupling, (jnp.int32(0), own_start)
     )
-    coupling = lax.psum(coupling_part, ("root", "virt", "occ"))
+    coupling = _manage_patches(coupling_part, ("virt", "occ"), "root")
     singles_fock = jnp.dot(singles_all, occ_fock, preferred_element_type=jnp.float32)
     singles_every = active[:, None] * (-singles_fock - 0.5 * coupling)
     sigma_singles = lax.dynamic_slice_in_dim(singles_every, root_index * local_roots, local_roots)

time: 599 us -> 621 us (1.037)
  blocking collectives: 50.7 us -> 71.7 us
    psum x1 -> x3, blocking collectives: 39.5 us -> 60.6 us  [the longest x1 36.8 us: local(): lax.psum(flat_pairs(trial_piece, sigma_piece), ('root', 'virt', 'occ'))]
  transfers between devices with their start and end apart: 8 -> 8, of which waited for: 4 -> 4; matrix products, arithmetic and copies ran while one was open for 37% -> 36% of each run, Pallas kernels for 0% -> 0%
where the time goes in v1:
time: 621 us; the launch traced here: 617 us
  waiting for transfers between devices  264 us (43%)
  local copies, waits for them, and re-layouts  192 us (31%)
  blocking collectives  71.7 us (12%)
  matrix products  36.1 us (6%)
  starting transfers between devices  28.4 us (5%)
  between operations  14.8 us (2%)
  other arithmetic  10.2 us (2%)
    all_to_all x1, waiting for transfers between devices, local(): lax.all_to_all(outer_part, 'root', split_axis=0, concat_axis=2, tiled=True)  180 us
    unnamed x23, local copies, waits for them, and re-layouts  74.1 us
    all_to_all x1, waiting for transfers between devices, local(): lax.all_to_all(trial_doubles, 'root', split_axis=2, concat_axis=0, tiled=...  40.7 us
    psum x1, blocking collectives, local(): lax.psum(flat_pairs(trial_piece, sigma_piece), ('root', 'virt', 'occ'))  36.8 us
    all_to_all x1, waiting for transfers between devices, local(): lax.all_to_all(gathered, 'root', split_axis=2, concat_axis=0, tiled=True)  31.6 us
    reshape x2, local copies, waits for them, and re-layouts, local(): stacked = gathered.reshape(batch_rows, occ_count, occ_count)  18.8 us
    dot_general x2, matrix products, flat_pairs(): lax.dot_general(left.reshape(left.shape[0], -1), right.reshape(right.shap...  14.6 us
    all_to_all x1, local copies, waits for them, and re-layouts, local(): lax.all_to_all(outer_part, 'root', split_axis=0, concat_axis=2, tiled=True)  14.6 us
  transfers between devices with their start and end apart: 8, of which 4 were waited for; matrix products, arithmetic and copies ran while one was open for 36% of the time, Pallas kernels for 0%

profile of v1, /device:TPU:0, one launch (start us, length us, event | category | flops | bytes accessed | tf_op | source)
XLA Modules:
  0.0 616.9 jit_solution(59587074410208663)
XLA Ops:
  7.2 6.9 %copy.53 = bf16[2,120,4608]{1,0,2:T(2,128)(2,1)} copy(bf16[2,120,4608]{2,1,0:T(8,128)(2,1)} %param.8) | data formatting | bytes 4423680 | tf_op args[1]
  14.1 5.2 all-to-all-start
  19.3 24.5 %copy.79 = bf16[6,8,120,2304]{3,1,2,0:T(8,128)(2,1)} copy(bf16[6,8,120,2304]{3,2,1,0:T(8,128)(2,1)} %bitcast.88) | data formatting | bytes 53084160
  43.7 11.1 %all-gather = bf16[4,2,96]{2,1,0:T(2,128)(2,1)S(1)} all-gather(bf16[1,2,96]{2,1,0:T(2,128)(2,1)S(1)} %bitcast.102), channel_id=1, replica_groups=mesh['root'=4,'virt'=4,'occ'=2] {'root'}, dimensions={0}, use_global_device_ids=true | all-gather | bytes 1920 | tf_op jit(solution)/shard_map/all_gather | solution.py:36
  54.9 10.4 %convolution_negate_fusion = f32[8,276480]{1,0:T(8,128)S(1)} fusion(bf16[48,276480]{1,0:T(8,128)(2,1)} %bitcast.84, bf16[8,96]{1,0:T(8,128)(2,1)S(1)} %bitcast.99, s32[]{:T(128)S(6)} %select_n.5), kind=kOutput, calls=%fused_computation | convolution fusion | flops 214548480 | bytes 35390980 | tf_op jit(solution)/shard_map/dot_general | solution.py:59
  65.3 6.1 copy.57
  71.5 5.7 all-to-all-start.2
  77.2 0.7 all-gather.3.cloned.1.call-update
  77.9 4.4 copy.54
  82.3 2.9 fusion.4
  85.3 3.1 copy.55
  88.3 180.0 %all-to-all-done.2 = f32[8,120,2304]{2,1,0:T(8,128)} async-done(((f32[8,120,2304]{2,1,0:T(8,128)}), f32[8,120,2304]{2,1,0:T(8,128)}, u32[]{:S(2)}, u32[]{:S(2)}) %all-to-all-start.2) | async-done | bytes 8847392 | tf_op jit(solution)/shard_map/all_to_all | solution.py:69
  268.3 3.9 all-to-all-start.1
  272.2 14.6 %copy.58 = f32[2,120,4,2304]{1,0,3,2:T(2,128)} copy(f32[2,120,4,2304]{3,1,0,2:T(8,128)} %bitcast.12) | data formatting | bytes 17694720 | tf_op jit(solution)/shard_map/all_to_all | solution.py:69
  286.8 10.8 %all-to-all-done.1 = bf16[2,480,1152]{2,0,1:T(2,128)(2,1)S(1)} async-done(((bf16[2,480,1152]{2,0,1:T(2,128)(2,1)}), bf16[2,480,1152]{2,0,1:T(2,128)(2,1)S(1)}, u32[]{:S(2)}, u32[]{:S(2)}) %all-to-all-start.1) | async-done | bytes 2211872 | tf_op jit(solution)/shard_map/all_to_all | solution.py:67
  297.6 1.4 copy-done.2
  298.9 3.7 all-to-all-start.5
  302.6 12.7 %copy.65 = bf16[2,120,9216]{1,0,2:T(2,128)(2,1)} copy(bf16[2,120,9216]{2,1,0:T(8,128)(2,1)} %all-gather.3.cloned.1.call-done) | data formatting | bytes 8847360 | tf_op jit(solution)/shard_map/all_gather | solution.py:37
  315.4 40.7 %all-to-all-done.5 = bf16[2,120,4608]{1,0,2:T(2,128)(2,1)S(1)} async-done(((bf16[2,120,4608]{1,0,2:T(2,128)(2,1)}), bf16[2,120,4608]{1,0,2:T(2,128)(2,1)S(1)}, u32[]{:S(2)}, u32[]{:S(2)}) %all-to-all-start.5) | async-done | bytes 2211872 | tf_op jit(solution)/shard_map/all_to_all | solution.py:74
  356.0 5.1 all-to-all-start.3
  361.2 5.9 reshape.49
  367.1 4.7 fusion.11
  371.8 7.2 %reshape.50 = f32[2,120,4608]{1,0,2:T(2,128)} reshape(f32[240,48,96]{0,2,1:T(8,128)} %fusion.11) | data formatting | bytes 8847360 | tf_op jit(solution)/shard_map/reshape | solution.py:47
  379.0 0.6 dynamic-slice
  380.3 8.9 %copy.56 = f32[2,4,120,1152]{2,0,3,1:T(2,128)} copy(bf16[2,4,120,1152]{3,0,2,1:T(2,128)(2,1)} %bitcast.95) | data formatting | bytes 6635520 | tf_op jit(solution)/shard_map/convert_element_type | solution.py:68
  389.2 9.5 %reshape.62 = bf16[240,96,96]{2,1,0:T(8,128)(2,1)} reshape(bf16[2,120,9216]{2,1,0:T(8,128)(2,1)} %all-gather.3.cloned.1.call-done) | data formatting | bytes 8847360 | tf_op jit(solution)/shard_map/reshape | solution.py:40
  398.7 9.3 %copy.61 = bf16[240,96,96]{0,1,2:T(8,128)(2,1)} copy(bf16[240,96,96]{2,1,0:T(8,128)(2,1)} %reshape.62) | data formatting | bytes 8847360 | tf_op jit(solution)/shard_map/reshape | solution.py:40
  408.0 3.2 convolution_bitcast_fusion
  411.2 4.8 copy.62
  416.0 7.1 %reshape.48 = f32[2,120,4608]{1,0,2:T(2,128)} reshape(f32[240,48,96]{0,2,1:T(8,128)} %copy.62) | data formatting | bytes 8847360 | tf_op jit(solution)/shard_map/reshape | solution.py:43
  423.2 10.2 %fusion.3 = bf16[2,120,4608]{1,0,2:T(2,128)(2,1)} fusion(f32[2,120,4608]{1,0,2:T(2,128)} %reshape.50, f32[2,120,4608]{1,0,2:T(2,128)} %reshape.48, f32[2,120,9216]{1,0,2:T(2,128)} %all-reduce.3.cloned.1.call-done, u32[]{:T(128)S(6)} %multiply.4, f32[2,4,120,1152]{2,0,3,1:T(2,128)} %copy.56, f32[2]{0:T(128)S(1)} %dynamic_slice.15), kind=kLoop, calls=%fused_computation.5 | loop fusion | flops 5529600 | bytes 19906572 | tf_op jit(solution)/shard_map/convert_element_type | solution.py:72
  433.4 31.6 %all-to-all-done.3 = bf16[2,120,9216]{1,0,2:T(2,128)(2,1)} async-done(((bf16[2,120,9216]{1,0,2:T(2,128)(2,1)}), bf16[2,120,9216]{1,0,2:T(2,128)(2,1)}, u32[]{:S(2)}, u32[]{:S(2)}) %all-to-all-start.3) | async-done | bytes 4423712 | tf_op jit(solution)/shard_map/all_to_all | solution.py:48
  465.0 4.7 all-to-all-start.4
  469.7 24.5 %copy.81 = bf16[6,8,120,2304]{3,1,2,0:T(8,128)(2,1)} copy(bf16[6,8,120,2304]{3,2,1,0:T(8,128)(2,1)} %bitcast.89) | data formatting | bytes 53084160
  494.2 4.3 copy.69
  498.5 1.9 copy.83
  500.4 12.2 %copy.66 = bf16[2,120,4,2304]{3,1,0,2:T(8,128)(2,1)} copy(bf16[2,120,4,2304]{1,0,3,2:T(2,128)(2,1)} %bitcast.17) | data formatting | bytes 8847360 | tf_op jit(solution)/shard_map/all_to_all | solution.py:48
  512.6 5.2 copy.80
  517.8 13.4 %fusion.17 = f32[8,48]{1,0:T(8,128)S(1)} fusion(bf16[8,276480]{1,0:T(8,128)(2,1)} %bitcast.87, bf16[48,276480]{1,0:T(8,128)(2,1)} %bitcast.83), kind=kOutput, calls=%fused_computation.27 | convolution fusion | flops 212336640 | bytes 30967296 | tf_op jit(solution)/shard_map/dot_general | solution.py:14
  531.4 11.9 %psum.21 = f32[8,96]{1,0:T(8,128)S(1)} all-reduce(f32[8,96]{1,0:T(8,128)S(1)} %dynamic_update_slice.3), channel_id=1, replica_groups=mesh['root'=4,'virt'=4,'occ'=2] {'virt','occ'}, use_global_device_ids=true, to_apply=%region_1.0 | all-reduce | flops 768 | bytes 6144 | tf_op jit(solution)/shard_map/psum | solution.py:9
  543.2 11.9 %psum.22 = f32[8,96]{1,0:T(8,128)S(1)} all-reduce(f32[8,96]{1,0:T(8,128)S(1)} %psum.21), channel_id=1, replica_groups=mesh['root'=4,'virt'=4,'occ'=2] {'root'}, use_global_device_ids=true, to_apply=%region_2.0 | all-reduce | flops 768 | bytes 6144 | tf_op jit(solution)/shard_map/psum | solution.py:10
  555.2 0.6 constant_dynamic-slice_fusion.1
  555.8 6.7 %copy.71 = bf16[2,120,4608]{2,1,0:T(8,128)(2,1)} copy(bf16[2,120,4608]{1,0,2:T(2,128)(2,1)} %fusion.3) | data formatting | bytes 4423680
  562.5 6.8 %copy.67 = bf16[2,120,4,1152]{3,1,0,2:T(8,128)(2,1)} copy(bf16[2,120,4,1152]{1,0,3,2:T(2,128)(2,1)} %bitcast.19) | data formatting | bytes 4423680 | tf_op jit(solution)/shard_map/all_to_all | solution.py:75
  569.3 1.9 copy.82
  571.2 1.2 convolution_bitcast_fusion.1
  572.4 36.8 %psum.23 = f32[8,8]{0,1:T(8,128)S(1)} all-reduce(f32[8,8]{0,1:T(8,128)S(1)} %convolution_bitcast_fusion.1), channel_id=1, replica_groups=mesh['root'=4,'virt'=4,'occ'=2] {'root','virt','occ'}, use_global_device_ids=true, to_apply=%region_3.0 | all-reduce | flops 64 | bytes 512 | tf_op jit(solution)/shard_map/psum | solution.py:77
  609.4 0.7 copy.72
  (27 shorter events, 0.6 us)
Async XLA Ops:
  7.2 75.2 %copy-start = (bf16[480,480]{1,0:T(8,128)(2,1)S(1)}, bf16[480,480]{1,0:T(8,128)(2,1)}, u32[]{:S(2)}) copy-start(bf16[480,480]{1,0:T(8,128)(2,1)} %param.10) | copy-start | bytes 1382404
  14.1 57.4 %all-to-all-start = ((bf16[2,120,4608]{1,0,2:T(2,128)(2,1)}), bf16[2,120,4608]{1,0,2:T(2,128)(2,1)S(1)}, u32[]{:S(2)}, u32[]{:S(2)}) async-start(bf16[2,120,4608]{1,0,2:T(2,128)(2,1)} %copy.53), calls=%async_computation | async-start | bytes 4718592 | tf_op jit(solution)/shard_map/all_to_all | solution.py:64
  19.3 24.5 %copy-start.4 = (bf16[2,96]{1,0:T(2,128)(2,1)S(1)}, bf16[2,96]{1,0:T(2,128)(2,1)}, u32[]{:S(2)}) copy-start(bf16[2,96]{1,0:T(2,128)(2,1)} %param.7) | copy-start | bytes 1156
  71.5 196.8 %all-to-all-start.2 = ((f32[8,120,2304]{2,1,0:T(8,128)}), f32[8,120,2304]{2,1,0:T(8,128)}, u32[]{:S(2)}, u32[]{:S(2)}) async-start(f32[8,120,2304]{2,1,0:T(8,128)} %copy.57), calls=%async_computation.2 | async-start | bytes 17694720 | tf_op jit(solution)/shard_map/all_to_all | solution.py:69
  77.2 225.4 %all-gather.3.cloned.1.call-start = ((), (), s32[]{:S(2)}) async-start(), calls=%async_computation.6 | async-start | bytes 6635520 | tf_op jit(solution)/shard_map/all_gather | solution.py:37
  268.3 29.2 %all-to-all-start.1 = ((bf16[2,480,1152]{2,0,1:T(2,128)(2,1)}), bf16[2,480,1152]{2,0,1:T(2,128)(2,1)S(1)}, u32[]{:S(2)}, u32[]{:S(2)}) async-start(bf16[2,480,1152]{2,0,1:T(2,128)(2,1)} %copy.55), calls=%async_computation.1 | async-start | bytes 4423680 | tf_op jit(solution)/shard_map/all_to_all | solution.py:67
  272.2 151.0 %all-reduce.3.cloned.1.call-start = ((), (), s32[]{:S(2)}) async-start(), calls=%async_computation.7 | async-start | bytes 18874368
  297.6 1.4 copy-start.2
  298.9 57.1 %all-to-all-start.5 = ((bf16[2,120,4608]{1,0,2:T(2,128)(2,1)}), bf16[2,120,4608]{1,0,2:T(2,128)(2,1)S(1)}, u32[]{:S(2)}, u32[]{:S(2)}) async-start(bf16[2,120,4608]{1,0,2:T(2,128)(2,1)} %copy.53), calls=%async_computation.5 | async-start | bytes 4718592 | tf_op jit(solution)/shard_map/all_to_all | solution.py:74
  356.0 108.9 %all-to-all-start.3 = ((bf16[2,120,9216]{1,0,2:T(2,128)(2,1)}), bf16[2,120,9216]{1,0,2:T(2,128)(2,1)}, u32[]{:S(2)}, u32[]{:S(2)}) async-start(bf16[2,120,9216]{1,0,2:T(2,128)(2,1)} %copy.65), calls=%async_computation.3 | async-start | bytes 9437184 | tf_op jit(solution)/shard_map/all_to_all | solution.py:48
  361.2 5.9 copy-start.3
  371.8 7.2 %copy-start.5 = (s32[8]{0:T(128)S(1)}, s32[8]{0:T(128)}, u32[]{:S(2)}) copy-start(s32[8]{0:T(128)} %param.13) | copy-start | bytes 100
  371.8 7.3 %copy-start.6 = (u32[32]{0:T(128)S(1)}, u32[32]{0:T(128)}, u32[]{:S(2)}) copy-start(u32[32]{0:T(128)} %constant.35) | copy-start | bytes 388
  465.0 97.5 %all-to-all-start.4 = ((bf16[2,120,4608]{1,0,2:T(2,128)(2,1)}), bf16[2,120,4608]{1,0,2:T(2,128)(2,1)}, u32[]{:S(2)}, u32[]{:S(2)}) async-start(bf16[2,120,4608]{1,0,2:T(2,128)(2,1)} %fusion.3), calls=%async_computation.4 | async-start | bytes 4718592 | tf_op jit(solution)/shard_map/all_to_all | solution.py:75
  562.5 47.6 %copy-start.1 = (bf16[480,480]{1,0:T(8,128)(2,1)S(1)}, bf16[480,480]{1,0:T(8,128)(2,1)}, u32[]{:S(2)}) copy-start(bf16[480,480]{1,0:T(8,128)(2,1)} %param.10) | copy-start | bytes 1382404
Sparse Core Ops, SparseCore 0:
  79.5 15.8 all-gather.2
  286.9 40.7 all-reduce.2
